TPU v7x, 32 devices: a whole 2x2x4 slice. The times are simulated.
32 devices in a mesh: grp: 2 (over core), row: 4 (over y, x), col: 4 (over z).
Axes of the slice: x: 2, y: 2, z: 4, core: 2. Of those that a mesh axis runs over, the one named last changes fastest.
Arguments:
- sub_rhs: float32 [2, 3, 4, 4, 256, 512], P('grp', None, 'row', 'col'), may hold values from -6 to 6
- sub_dinv: float32 [2, 3, 4, 4, 256, 256], P('grp', None, 'row', 'col')
- anc_rhs: float32 [4, 4, 256, 512], P('row', 'col'), may hold values from -6 to 6
- anc_dinv: float32 [4, 4, 256, 256], P('row', 'col')
- tiles: bfloat16 [2, 4, 4, 3, 16, 256, 256], P('grp', 'row', 'col'), may hold values from -0.09375 to 0.09375
- tile_target: int32 [2, 4, 4, 3, 16], P('grp', 'row', 'col'), may hold values from 0 to 11, as said below
- tile_source: int32 [2, 4, 4, 3, 16], P('grp', 'row', 'col'), may hold values from 0 to 3, as said below
- tile_count: int32 [2, 4, 4, 3], P('grp', 'row', 'col'), may hold values from 1 to 16, as said below
Outputs:
- sub_solution: float32 [2, 3, 4, 4, 256, 512], P('grp', None, 'row', 'col')
- anc_solution: float32 [4, 4, 256, 512], P('row', 'col')
Inputs may be any that keep to these rules, and one draw needn't show every extreme that they name: `tile_target`: entry [g, q, c, k, j] is (t - 1) * 4 + r for a target level t with k < t <= 3 (t = 3 is the ancestor level) and a process row r; entries at slots j >= tile_count are unused. `tile_source`: Non-decreasing along the last dimension. `tile_count`: for every source level some device holds exactly 16 live tiles.
All inputs are finite; a program needn't handle non-finite values.
Results may differ from a plain program's by a relative error of at most 0.0027.
Values may be sent and summed in bfloat16 or wider, within the bound.
A program may use at most 128 MiB of HBM per device.

v0:
```python
import functools

import jax
import jax.numpy as jnp
from jax import lax
from jax.experimental import pallas as pl
from jax.experimental.pallas import tpu as pltpu
from jax.sharding import PartitionSpec as P

MESH = pl.DeviceIdType.MESH
CHUNK = 128
AHEAD = 2
LAG = 1


def kernel(
    n_grp, n_row, n_col,
    target_ref, source_ref, count_ref,
    rhs_hbm, inv_hbm, anc_rhs_hbm, anc_inv_hbm, tiles_hbm,
    sub_out, anc_out,
    rhs, inv, anc_rhs, anc_inv, tiles,
    gathered, fetched, chain, pending, outbox, inbox, anc_box,
    prev_s, last_s, src_s,
    load_sem, ag_send, ag_recv, fwd_send, rs_send, rs_recv, anc_send, anc_recv,
):
    depth, size, width = rhs.shape
    slots = tiles.shape[1]
    chunks = width // CHUNK
    steps = depth * chunks
    codes = depth * n_row
    g = lax.axis_index("grp")
    q = lax.axis_index("row")
    c = lax.axis_index("col")

    early = [
        pltpu.make_async_copy(inv_hbm.at[0], inv.at[0], load_sem.at[0]),
        pltpu.make_async_copy(rhs_hbm.at[0], rhs.at[0], load_sem.at[1]),
    ]
    loads = [
        pltpu.make_async_copy(tiles_hbm, tiles, load_sem.at[2]),
        pltpu.make_async_copy(anc_rhs_hbm, anc_rhs, load_sem.at[3]),
        pltpu.make_async_copy(anc_inv_hbm, anc_inv, load_sem.at[4]),
    ]
    if depth > 1:
        loads += [
            pltpu.make_async_copy(inv_hbm.at[pl.ds(1, depth - 1)], inv.at[pl.ds(1, depth - 1)], load_sem.at[5]),
            pltpu.make_async_copy(rhs_hbm.at[pl.ds(1, depth - 1)], rhs.at[pl.ds(1, depth - 1)], load_sem.at[6]),
        ]
    for load in early:
        load.start()

    barrier = pltpu.get_barrier_semaphore()
    for d in range(1, n_col):
        pl.semaphore_signal(barrier, inc=1, device_id=(g, q, lax.rem(c + d, n_col)), device_id_type=MESH)
    for e in range(n_grp):
        for d in range(n_row):
            if e or d:
                pl.semaphore_signal(
                    barrier, inc=1,
                    device_id=(lax.rem(g + e, n_grp), lax.rem(q + d, n_row), c), device_id_type=MESH,
                )

    def tables(k, carry):
        count = count_ref[0, 0, 0, k]
        raw = [target_ref[k, 0, j] for j in range(slots)]
        live = [jnp.where(j < count, raw[j], -1) for j in range(slots)]
        for j in range(slots):
            found = jnp.int32(0)
            for i in range(j):
                found = jnp.where(raw[i] == raw[j], i + 1, found)
            prev_s[k * slots + j] = found
            src_s[k * slots + j] = jnp.clip(source_ref[k, 0, j], 0, n_col - 1)
        for code in range(codes):
            found = jnp.int32(0)
            for j in range(slots):
                found = jnp.where(live[j] == code, j + 1, found)
            last_s[k * codes + code] = found
        return carry

    def cols(w):
        return pl.ds(pl.multiple_of(w * CHUNK, CHUNK), CHUNK)

    def ag_copy(i, owner, peer):
        return pltpu.make_async_remote_copy(
            src_ref=gathered.at[i, owner], dst_ref=gathered.at[i, owner],
            send_sem=ag_send.at[i, peer], recv_sem=ag_recv.at[i, owner],
            device_id=(g, q, peer), device_id_type=MESH,
        )

    def relays(i, run):
        for way, (owner, relay, end) in enumerate(((0, n_col - 2, n_col - 1), (n_col - 1, 1, 0))):
            if n_col > 2:

                @pl.when(c == relay)
                def _():
                    run(
                        ag_copy(i, owner, c),
                        pltpu.make_async_remote_copy(
                            src_ref=gathered.at[i, owner], dst_ref=gathered.at[i, owner],
                            send_sem=fwd_send.at[i, way], recv_sem=ag_recv.at[i, owner],
                            device_id=(g, q, end), device_id_type=MESH,
                        ),
                    )

    def each_direct(i, run):
        for d in range(1, n_col):
            peer = lax.rem(c + d, n_col)
            far = (n_col > 2) & (jnp.abs(peer - c) == n_col - 1)

            @pl.when(jnp.logical_not(far))
            def _():
                run(ag_copy(i, c, peer), held(i, peer))

    def held(i, peer):
        if n_col <= 2:
            return False
        to_end = ((c == n_col - 2) & (peer == n_col - 1)) | ((c == 1) & (peer == 0))
        return to_end & (i >= AHEAD) & (i < chunks)

    def send_direct(i):
        def start(copy, wait_turn):
            pl.when(jnp.logical_not(wait_turn))(copy.start)

        each_direct(i, start)

    def release(i):
        for relay, end in ((n_col - 2, n_col - 1), (1, 0)):
            if n_col > 2:

                @pl.when((c == relay) & (i + AHEAD < chunks))
                def _():
                    ag_copy(i + AHEAD, c, end).start()

    def rs_copy(i, owner_g, owner_q, to_g, to_q):
        return pltpu.make_async_remote_copy(
            src_ref=outbox.at[i, to_q], dst_ref=inbox.at[i, owner_g * n_row + owner_q],
            send_sem=rs_send.at[i, to_q], recv_sem=rs_recv.at[i, owner_g * n_row + owner_q],
            device_id=(to_g, to_q, c), device_id_type=MESH,
        )

    def anc_copy(w, peer_g):
        return pltpu.make_async_remote_copy(
            src_ref=anc_box.at[w], dst_ref=anc_box.at[w],
            send_sem=anc_send.at[w, peer_g], recv_sem=anc_recv.at[w],
            device_id=(peer_g, q, c), device_id_type=MESH,
        )

    def full_dot(a, b):
        return jnp.dot(a, b, precision=lax.Precision.HIGHEST, preferred_element_type=jnp.float32)

    def solve(i, k, w, first):
        rest = rhs[k, :, cols(w)]
        if not first:
            back = i - chunks
            total = pending[w, (k - 1) * n_row + q]
            for d in range(1, n_row):
                other = lax.rem(q + d, n_row)
                rs_copy(back, g, other, g, q).wait_recv()
                total = total + inbox[back, g * n_row + other].astype(jnp.float32)
            rest = rest - total
        answer = full_dot(inv[k], rest)
        sub_out[k, :, cols(w)] = answer
        gathered[i, c] = answer.astype(jnp.bfloat16)

    def pass_on(arrived, onward):
        arrived.wait_recv()
        onward.start()

    def spread(i, k, w):
        relays(i, pass_on)
        release(i)
        for d in range(1, n_col):
            other = lax.rem(c + d, n_col)
            passed = False
            if n_col > 2:
                passed = ((c == n_col - 2) & (other == 0)) | ((c == 1) & (other == n_col - 1))

            @pl.when(jnp.logical_not(passed))
            def _():
                ag_copy(i, other, c).wait_recv()

        for s in range(n_col):
            fetched[s] = gathered[i, s]

        for j in range(slots):
            product = jnp.dot(
                tiles[k, j], fetched[src_s[k * slots + j]], preferred_element_type=jnp.float32
            )
            chain[j + 1] = product + chain[prev_s[k * slots + j]]

        def updated(code):
            return pending[w, code] + chain[last_s[k * codes + code]]

        to_g = jnp.where(k < depth - 1, g, lax.rem(w, n_grp))
        for d in list(range(1, n_row)) + [0]:
            to_q = lax.rem(q + d, n_row)
            value = updated(k * n_row + to_q)

            def send():
                outbox[i, to_q] = value.astype(jnp.bfloat16)
                rs_copy(i, g, q, to_g, to_q).start()

            if d == 0:
                pending[w, k * n_row + q] = value
                pl.when(to_g != g)(send)
            else:
                send()

        def collect(code, carry):
            pending[w, code] = updated(code)
            return carry

        lax.fori_loop((k + 1) * n_row, codes, collect, 0)

    def finish(w):
        i = (depth - 1) * chunks + w

        @pl.when(lax.rem(w, n_grp) == g)
        def _():
            total = pending[w, (depth - 1) * n_row + q]
            for e in range(n_grp):
                for d in range(n_row):
                    if e or d:
                        other_g, other_q = lax.rem(g + e, n_grp), lax.rem(q + d, n_row)
                        rs_copy(i, other_g, other_q, g, q).wait_recv()
                        total = total + inbox[i, other_g * n_row + other_q].astype(jnp.float32)
            anc_box[w] = full_dot(anc_inv[...], anc_rhs[:, cols(w)] - total)
            for e in range(1, n_grp):
                anc_copy(w, lax.rem(g + e, n_grp)).start()

    for load in early:
        load.wait()
    for load in loads:
        load.start()
    solve(0, 0, 0, True)
    pl.semaphore_wait(barrier, n_col - 1 + n_grp * n_row - 1)

    send_direct(0)

    def first_level(w, carry):
        solve(w, 0, w, True)
        send_direct(w)
        return carry

    lax.fori_loop(1, chunks, first_level, 0)
    lax.fori_loop(0, depth, tables, 0)
    chain[0] = jnp.zeros(chain.shape[1:], jnp.float32)

    def clear(n, carry):
        pending[n // codes, lax.rem(n, codes)] = jnp.zeros(pending.shape[2:], jnp.float32)
        return carry

    lax.fori_loop(0, chunks * codes, clear, 0)
    for load in loads:
        load.wait()

    def middle(i, carry):
        spread(i, i // chunks, lax.rem(i, chunks))
        later = i + chunks - LAG

        @pl.when((i >= LAG) & (later < steps))
        def _():
            solve(later, later // chunks, lax.rem(later, chunks), False)
            send_direct(later)

        @pl.when(later >= steps)
        def _():
            finish(later - steps)

        return carry

    lax.fori_loop(0, steps, middle, 0)
    for w in range(chunks - LAG, chunks):
        finish(jnp.int32(w))

    def deliver(w, carry):
        owner = lax.rem(w, n_grp)

        @pl.when(owner != g)
        def _():
            anc_copy(w, g).wait_recv()

        anc_out[:, cols(w)] = anc_box[w]

        @pl.when(owner == g)
        def _():
            for e in range(1, n_grp):
                anc_copy(w, lax.rem(g + e, n_grp)).wait_send()

        return carry

    lax.fori_loop(0, chunks, deliver, 0)

    def drain(i, carry):
        each_direct(i, lambda copy, wait_turn: copy.wait_send())
        relays(i, lambda arrived, onward: onward.wait_send())
        to_g = jnp.where(i < (depth - 1) * chunks, g, lax.rem(lax.rem(i, chunks), n_grp))
        for d in range(1, n_row):
            rs_copy(i, g, q, to_g, lax.rem(q + d, n_row)).wait_send()

        @pl.when(to_g != g)
        def _():
            rs_copy(i, g, q, to_g, q).wait_send()

        return carry

    lax.fori_loop(0, steps, drain, 0)


def on_device(mesh, sub_rhs, sub_dinv, anc_rhs, anc_dinv, tiles, tile_target, tile_source, tile_count):
    n_grp, n_row, n_col = mesh.shape["grp"], mesh.shape["row"], mesh.shape["col"]
    depth, size, width = sub_rhs.shape[1], sub_rhs.shape[4], sub_rhs.shape[5]
    slots = tiles.shape[4]
    chunks = width // CHUNK
    steps = depth * chunks
    codes = depth * n_row
    bf16, f32 = jnp.bfloat16, jnp.float32
    dma = pltpu.SemaphoreType.DMA
    sub, anc = pl.pallas_call(
        functools.partial(kernel, n_grp, n_row, n_col),
        out_shape=(
            jax.ShapeDtypeStruct((depth, size, width), f32),
            jax.ShapeDtypeStruct((size, width), f32),
        ),
        in_specs=[pl.BlockSpec(memory_space=pltpu.SMEM)] * 3 + [pl.BlockSpec(memory_space=pl.ANY)] * 5,
        out_specs=(pl.BlockSpec(memory_space=pltpu.VMEM), pl.BlockSpec(memory_space=pltpu.VMEM)),
        scratch_shapes=[
            pltpu.VMEM((depth, size, width), f32),
            pltpu.VMEM((depth, size, size), f32),
            pltpu.VMEM((size, width), f32),
            pltpu.VMEM((size, size), f32),
            pltpu.VMEM((depth, slots, size, size), bf16),
            pltpu.VMEM((steps, n_col, size, CHUNK), bf16),
            pltpu.VMEM((n_col, size, CHUNK), bf16),
            pltpu.VMEM((slots + 1, size, CHUNK), f32),
            pltpu.VMEM((chunks, codes, size, CHUNK), f32),
            pltpu.VMEM((steps, n_row, size, CHUNK), bf16),
            pltpu.VMEM((steps, n_grp * n_row, size, CHUNK), bf16),
            pltpu.VMEM((chunks, size, CHUNK), f32),
            pltpu.SMEM((depth * slots,), jnp.int32),
            pltpu.SMEM((depth * codes,), jnp.int32),
            pltpu.SMEM((depth * slots,), jnp.int32),
            dma((7,)),
            dma((steps, n_col)),
            dma((steps, n_col)),
            dma((steps, 2)),
            dma((steps, n_row)),
            dma((steps, n_grp * n_row)),
            dma((chunks, n_grp)),
            dma((chunks,)),
        ],
        compiler_params=pltpu.CompilerParams(
            collective_id=0, has_side_effects=True, vmem_limit_bytes=67_043_328
        ),
    )(
        tile_target.reshape(depth, 1, slots), tile_source.reshape(depth, 1, slots), tile_count,
        sub_rhs.reshape(depth, size, width), sub_dinv.reshape(depth, size, size),
        anc_rhs.reshape(size, width), anc_dinv.reshape(size, size),
        tiles.reshape(depth, slots, size, size),
    )
    return sub[None, :, None, None], anc[None, None]


def solution(mesh):
    placed = (
        P("grp", None, "row", "col", None, None),
        P("grp", None, "row", "col", None, None),
        P("row", "col", None, None),
        P("row", "col", None, None),
        P("grp", "row", "col", None, None, None, None),
        P("grp", "row", "col", None, None),
        P("grp", "row", "col", None, None),
        P("grp", "row", "col", None),
    )
    return jax.shard_map(
        functools.partial(on_device, mesh),
        mesh=mesh,
        in_specs=placed,
        out_specs=(P("grp", None, "row", "col", None, None), P("row", "col", None, None)),
        check_vma=False,
    )
```

profile of v0, /device:TPU:0, one launch (start us, length us, event | category | flops | bytes accessed | tf_op | source)
XLA Modules:
  0.0 78.0 jit_solution(7449050388005393090)
XLA Ops:
  0.6 73.8 %shard_map.95 = (f32[3,256,512]{2,1,0:T(8,128)}, f32[256,512]{1,0:T(8,128)}) custom-call(s32[3,1,16]{2,1,0:T(1,128)} %bitcast.18, s32[3,1,16]{2,1,0:T(1,128)} %bitcast.19, s32[1,1,1,3]{3,2,1,0:T(1,128)} %count_ref.1, f32[3,256,512]{2,1,0:T(8,128)} %bitcast.13, f32[3,256,256]{2,1,0:T(8,128)} %bitcast.14, f32[256,512]{1,0:T(8,128)} %bitcast.15, ...), custom_call_target="tpu_custom_call" | custom-call | tf_op jit(solution)/shard_map/pallas_call | solution.py:319
  74.4 0.0 copy-start
  74.4 2.7 %copy.13 = f32[1,3,1,1,256,512]{5,4,3,2,1,0:T(8,128)} copy(f32[1,3,1,1,256,512]{5,4,3,2,1,0:T(8,128)} %bitcast.12) | data formatting | bytes 3145728
  77.2 0.0 copy-done
  77.2 0.8 %copy.14 = f32[1,1,256,512]{3,2,1,0:T(8,128)} copy(f32[1,1,256,512]{3,2,1,0:T(8,128)S(1)} %bitcast.16) | data formatting | bytes 1048576
Async XLA Ops:
  74.4 2.7 %copy-start = (f32[256,512]{1,0:T(8,128)S(1)}, f32[256,512]{1,0:T(8,128)}, u32[]{:S(2)}) copy-start(f32[256,512]{1,0:T(8,128)} %get-tuple-element.5) | copy-start | bytes 1572868
where the time goes:
time: 78.2 us; the launch traced here: 78 us
  Pallas kernels  73.8 us (94%)
  local copies, waits for them, and re-layouts  3.52 us (5%)
    pallas_call x1, Pallas kernels, on_device(): pl.pallas_call(functools.partial(kernel, n_grp, n_row, n_col), out_shape=...  73.8 us
    unnamed x4, local copies, waits for them, and re-layouts  3.52 us

commit v1 on v0

--- a/solution.py
+++ b/solution.py
@@ -9,18 +9,26 @@
 
 MESH = pl.DeviceIdType.MESH
 CHUNK = 128
-AHEAD = 2
+AHEAD = 3
 LAG = 1
+
+
+def hops(n_col):
+    if not 2 < n_col <= 4:
+        return ()
+    up = [(o, n_col - 2, n_col - 1) for o in reversed(range(n_col - 2))]
+    down = [(o, 1, 0) for o in range(2, n_col)]
+    return tuple(up + down)
 
 
 def kernel(
     n_grp, n_row, n_col,
-    target_ref, source_ref, count_ref,
+    target_hbm, source_hbm, count_hbm,
     rhs_hbm, inv_hbm, anc_rhs_hbm, anc_inv_hbm, tiles_hbm,
     sub_out, anc_out,
     rhs, inv, anc_rhs, anc_inv, tiles,
     gathered, fetched, chain, pending, outbox, inbox, anc_box,
-    prev_s, last_s, src_s,
+    target_ref, source_ref, count_ref, prev_s, last_s, src_s,
     load_sem, ag_send, ag_recv, fwd_send, rs_send, rs_recv, anc_send, anc_recv,
 ):
     depth, size, width = rhs.shape
@@ -28,6 +36,7 @@
     chunks = width // CHUNK
     steps = depth * chunks
     codes = depth * n_row
+    passes = hops(n_col)
     g = lax.axis_index("grp")
     q = lax.axis_index("row")
     c = lax.axis_index("col")
@@ -35,6 +44,11 @@
     early = [
         pltpu.make_async_copy(inv_hbm.at[0], inv.at[0], load_sem.at[0]),
         pltpu.make_async_copy(rhs_hbm.at[0], rhs.at[0], load_sem.at[1]),
+    ]
+    maps = [
+        pltpu.make_async_copy(target_hbm, target_ref, load_sem.at[7]),
+        pltpu.make_async_copy(source_hbm, source_ref, load_sem.at[8]),
+        pltpu.make_async_copy(count_hbm, count_ref, load_sem.at[9]),
     ]
     loads = [
         pltpu.make_async_copy(tiles_hbm, tiles, load_sem.at[2]),
@@ -50,8 +64,18 @@
         load.start()
 
     barrier = pltpu.get_barrier_semaphore()
+    apart = [(o, e) for o, _, e in passes if (e, o) in [(a, b) for a, _, b in passes]]
+    strangers = sum((c == o).astype(jnp.int32) for o, _ in apart) if apart else 0
     for d in range(1, n_col):
-        pl.semaphore_signal(barrier, inc=1, device_id=(g, q, lax.rem(c + d, n_col)), device_id_type=MESH)
+        peer = lax.rem(c + d, n_col)
+        met = True
+        for o, e in apart:
+            met = met & jnp.logical_not((c == o) & (peer == e))
+
+        @pl.when(met)
+        def _():
+            pl.semaphore_signal(barrier, inc=1, device_id=(g, q, peer), device_id_type=MESH)
+
     for e in range(n_grp):
         for d in range(n_row):
             if e or d:
@@ -88,31 +112,32 @@
         )
 
     def relays(i, run):
-        for way, (owner, relay, end) in enumerate(((0, n_col - 2, n_col - 1), (n_col - 1, 1, 0))):
-            if n_col > 2:
-
-                @pl.when(c == relay)
-                def _():
-                    run(
-                        ag_copy(i, owner, c),
-                        pltpu.make_async_remote_copy(
-                            src_ref=gathered.at[i, owner], dst_ref=gathered.at[i, owner],
-                            send_sem=fwd_send.at[i, way], recv_sem=ag_recv.at[i, owner],
-                            device_id=(g, q, end), device_id_type=MESH,
-                        ),
-                    )
+        for way, (owner, relay, end) in enumerate(passes):
+
+            @pl.when(c == relay)
+            def _():
+                run(
+                    ag_copy(i, owner, c),
+                    pltpu.make_async_remote_copy(
+                        src_ref=gathered.at[i, owner], dst_ref=gathered.at[i, owner],
+                        send_sem=fwd_send.at[i, way], recv_sem=ag_recv.at[i, owner],
+                        device_id=(g, q, end), device_id_type=MESH,
+                    ),
+                )
 
     def each_direct(i, run):
         for d in range(1, n_col):
             peer = lax.rem(c + d, n_col)
-            far = (n_col > 2) & (jnp.abs(peer - c) == n_col - 1)
+            far = False
+            for owner, relay, end in passes:
+                far = far | ((c == owner) & (peer == end))
 
             @pl.when(jnp.logical_not(far))
             def _():
                 run(ag_copy(i, c, peer), held(i, peer))
 
     def held(i, peer):
-        if n_col <= 2:
+        if not passes:
             return False
         to_end = ((c == n_col - 2) & (peer == n_col - 1)) | ((c == 1) & (peer == 0))
         return to_end & (i >= AHEAD) & (i < chunks)
@@ -125,7 +150,7 @@
 
     def release(i):
         for relay, end in ((n_col - 2, n_col - 1), (1, 0)):
-            if n_col > 2:
+            if passes:
 
                 @pl.when((c == relay) & (i + AHEAD < chunks))
                 def _():
@@ -172,8 +197,8 @@
         for d in range(1, n_col):
             other = lax.rem(c + d, n_col)
             passed = False
-            if n_col > 2:
-                passed = ((c == n_col - 2) & (other == 0)) | ((c == 1) & (other == n_col - 1))
+            for owner, relay, end in passes:
+                passed = passed | ((c == relay) & (other == owner))
 
             @pl.when(jnp.logical_not(passed))
             def _():
@@ -230,10 +255,10 @@
 
     for load in early:
         load.wait()
-    for load in loads:
+    for load in maps + loads:
         load.start()
     solve(0, 0, 0, True)
-    pl.semaphore_wait(barrier, n_col - 1 + n_grp * n_row - 1)
+    pl.semaphore_wait(barrier, n_col - 1 + n_grp * n_row - 1 - strangers)
 
     send_direct(0)
 
@@ -243,6 +268,8 @@
         return carry
 
     lax.fori_loop(1, chunks, first_level, 0)
+    for load in maps:
+        load.wait()
     lax.fori_loop(0, depth, tables, 0)
     chain[0] = jnp.zeros(chain.shape[1:], jnp.float32)
 
@@ -305,6 +332,17 @@
         return carry
 
     lax.fori_loop(0, steps, drain, 0)
+
+
+def hand_over(sub_ref, anc_ref, sub_out, anc_out, sem):
+    copies = [
+        pltpu.make_async_copy(sub_ref, sub_out, sem.at[0]),
+        pltpu.make_async_copy(anc_ref, anc_out, sem.at[1]),
+    ]
+    for copy in copies:
+        copy.start()
+    for copy in copies:
+        copy.wait()
 
 
 def on_device(mesh, sub_rhs, sub_dinv, anc_rhs, anc_dinv, tiles, tile_target, tile_source, tile_count):
@@ -319,10 +357,10 @@
     sub, anc = pl.pallas_call(
         functools.partial(kernel, n_grp, n_row, n_col),
         out_shape=(
-            jax.ShapeDtypeStruct((depth, size, width), f32),
-            jax.ShapeDtypeStruct((size, width), f32),
+            pltpu.VMEM((depth, size, width), f32),
+            pltpu.VMEM((size, width), f32),
         ),
-        in_specs=[pl.BlockSpec(memory_space=pltpu.SMEM)] * 3 + [pl.BlockSpec(memory_space=pl.ANY)] * 5,
+        in_specs=[pl.BlockSpec(memory_space=pltpu.HBM)] * 8,
         out_specs=(pl.BlockSpec(memory_space=pltpu.VMEM), pl.BlockSpec(memory_space=pltpu.VMEM)),
         scratch_shapes=[
             pltpu.VMEM((depth, size, width), f32),
@@ -337,20 +375,23 @@
             pltpu.VMEM((steps, n_row, size, CHUNK), bf16),
             pltpu.VMEM((steps, n_grp * n_row, size, CHUNK), bf16),
             pltpu.VMEM((chunks, size, CHUNK), f32),
+            pltpu.SMEM((depth, 1, slots), jnp.int32),
+            pltpu.SMEM((depth, 1, slots), jnp.int32),
+            pltpu.SMEM((1, 1, 1, depth), jnp.int32),
             pltpu.SMEM((depth * slots,), jnp.int32),
             pltpu.SMEM((depth * codes,), jnp.int32),
             pltpu.SMEM((depth * slots,), jnp.int32),
-            dma((7,)),
+            dma((10,)),
             dma((steps, n_col)),
             dma((steps, n_col)),
-            dma((steps, 2)),
+            dma((steps, max(len(hops(n_col)), 1))),
             dma((steps, n_row)),
             dma((steps, n_grp * n_row)),
             dma((chunks, n_grp)),
             dma((chunks,)),
         ],
         compiler_params=pltpu.CompilerParams(
-            collective_id=0, has_side_effects=True, vmem_limit_bytes=67_043_328
+            collective_id=0, has_side_effects=True, vmem_limit_bytes=67_043_328 - 4 * (depth + 1) * size * width
         ),
     )(
         tile_target.reshape(depth, 1, slots), tile_source.reshape(depth, 1, slots), tile_count,
@@ -358,6 +399,17 @@
         anc_rhs.reshape(size, width), anc_dinv.reshape(size, size),
         tiles.reshape(depth, slots, size, size),
     )
+    sub, anc = pl.pallas_call(
+        hand_over,
+        out_shape=(
+            jax.ShapeDtypeStruct((depth, size, width), f32),
+            jax.ShapeDtypeStruct((size, width), f32),
+        ),
+        in_specs=[pl.BlockSpec(memory_space=pl.ANY)] * 2,
+        out_specs=(pl.BlockSpec(memory_space=pl.ANY), pl.BlockSpec(memory_space=pl.ANY)),
+        scratch_shapes=[dma((2,))],
+        compiler_params=pltpu.CompilerParams(vmem_limit_bytes=1 << 20),
+    )(sub, anc)
     return sub[None, :, None, None], anc[None, None]
 
 

time: 78.2 us -> 71.3 us (0.912)
  local copies, waits for them, and re-layouts: 3.52 us -> 0 us
  Pallas kernels: 73.8 us -> 70.5 us
    pallas_call x1, Pallas kernels: 73.8 us -> 69.1 us  [on_device(): pl.pallas_call(functools.partial(kernel, n_grp, n_row, n_col), out_shape=...]
    unnamed x4 -> x0, local copies, waits for them, and re-layouts: 3.52 us -> none
    pallas_call x0 -> x1, Pallas kernels: none -> 1.33 us  [on_device(): pl.pallas_call(hand_over, out_shape=(jax.ShapeDtypeStruct((depth, size, w...]
where the time goes in v1:
time: 71.3 us; the launch traced here: 71.1 us
  Pallas kernels  70.5 us (99%)
    pallas_call x1, Pallas kernels, on_device(): pl.pallas_call(functools.partial(kernel, n_grp, n_row, n_col), out_shape=...  69.1 us

profile of v1, /device:TPU:0, one launch (start us, length us, event | category | flops | bytes accessed | tf_op | source)
XLA Modules:
  0.0 71.1 jit_solution(251534484569324698)
XLA Ops:
  0.6 69.1 %shard_map.95 = (f32[3,256,512]{2,1,0:T(8,128)S(1)}, f32[256,512]{1,0:T(8,128)S(1)}) custom-call(s32[3,1,16]{2,1,0:T(1,128)} %bitcast.16, s32[3,1,16]{2,1,0:T(1,128)} %bitcast.17, s32[1,1,1,3]{3,2,1,0:T(1,128)} %count_hbm.1, f32[3,256,512]{2,1,0:T(8,128)} %bitcast.12, f32[3,256,256]{2,1,0:T(8,128)} %bitcast.13, f32[256,512]{1,0:T(8,128)} %bitcast.14, ...), custom_call_target="tpu_custom_call" | custom-call | tf_op jit(solution)/shard_map/pallas_call | solution.py:357
  69.8 1.3 %shard_map.96 = (f32[3,256,512]{2,1,0:T(8,128)}, f32[256,512]{1,0:T(8,128)}) custom-call(f32[3,256,512]{2,1,0:T(8,128)S(1)} %get-tuple-element.6.sub_ref, f32[256,512]{1,0:T(8,128)S(1)} %get-tuple-element.7.anc_ref), custom_call_target="tpu_custom_call" | custom-call | tf_op jit(solution)/shard_map/pallas_call | solution.py:402

commit v2 on v1

--- a/solution.py
+++ b/solution.py
@@ -192,8 +192,6 @@
         onward.start()
 
     def spread(i, k, w):
-        relays(i, pass_on)
-        release(i)
         for d in range(1, n_col):
             other = lax.rem(c + d, n_col)
             passed = False
@@ -283,6 +281,12 @@
 
     def middle(i, carry):
         spread(i, i // chunks, lax.rem(i, chunks))
+
+        @pl.when(i + 1 < steps)
+        def _():
+            relays(i + 1, pass_on)
+            release(i + 1)
+
         later = i + chunks - LAG
 
         @pl.when((i >= LAG) & (later < steps))
@@ -296,6 +300,8 @@
 
         return carry
 
+    relays(0, pass_on)
+    release(0)
     lax.fori_loop(0, steps, middle, 0)
     for w in range(chunks - LAG, chunks):
         finish(jnp.int32(w))

time: 71.3 us -> 70.1 us (0.983)
  Pallas kernels: 70.5 us -> 69.3 us
    pallas_call x1, Pallas kernels: 69.1 us -> 68 us  [on_device(): pl.pallas_call(functools.partial(kernel, n_grp, n_row, n_col), out_shape=...]
where the time goes in v2:
time: 70.1 us; the launch traced here: 70 us
  Pallas kernels  69.3 us (99%)
    pallas_call x1, Pallas kernels, on_device(): pl.pallas_call(functools.partial(kernel, n_grp, n_row, n_col), out_shape=...  68 us

profile of v2, /device:TPU:0, one launch (start us, length us, event | category | flops | bytes accessed | tf_op | source)
XLA Modules:
  0.0 70.0 jit_solution(9203694867595904237)
XLA Ops:
  0.6 68.0 %shard_map.95 = (f32[3,256,512]{2,1,0:T(8,128)S(1)}, f32[256,512]{1,0:T(8,128)S(1)}) custom-call(s32[3,1,16]{2,1,0:T(1,128)} %bitcast.16, s32[3,1,16]{2,1,0:T(1,128)} %bitcast.17, s32[1,1,1,3]{3,2,1,0:T(1,128)} %count_hbm.1, f32[3,256,512]{2,1,0:T(8,128)} %bitcast.12, f32[3,256,256]{2,1,0:T(8,128)} %bitcast.13, f32[256,512]{1,0:T(8,128)} %bitcast.14, ...), custom_call_target="tpu_custom_call" | custom-call | tf_op jit(solution)/shard_map/pallas_call | solution.py:363
  68.6 1.3 %shard_map.96 = (f32[3,256,512]{2,1,0:T(8,128)}, f32[256,512]{1,0:T(8,128)}) custom-call(f32[3,256,512]{2,1,0:T(8,128)S(1)} %get-tuple-element.6.sub_ref, f32[256,512]{1,0:T(8,128)S(1)} %get-tuple-element.7.anc_ref), custom_call_target="tpu_custom_call" | custom-call | tf_op jit(solution)/shard_map/pallas_call | solution.py:408

commit v3 on v2

--- a/solution.py
+++ b/solution.py
@@ -11,6 +11,7 @@
 CHUNK = 128
 AHEAD = 3
 LAG = 1
+BEHIND = 3
 
 
 def hops(n_col):
@@ -29,7 +30,7 @@
     rhs, inv, anc_rhs, anc_inv, tiles,
     gathered, fetched, chain, pending, outbox, inbox, anc_box,
     target_ref, source_ref, count_ref, prev_s, last_s, src_s,
-    load_sem, ag_send, ag_recv, fwd_send, rs_send, rs_recv, anc_send, anc_recv,
+    load_sem, ag_send, ag_recv, fwd_send, rs_send, rs_recv, anc_send, anc_recv, plane_sem,
 ):
     depth, size, width = rhs.shape
     slots = tiles.shape[1]
@@ -43,8 +44,10 @@
 
     early = [
         pltpu.make_async_copy(inv_hbm.at[0], inv.at[0], load_sem.at[0]),
-        pltpu.make_async_copy(rhs_hbm.at[0], rhs.at[0], load_sem.at[1]),
+        pltpu.make_async_copy(rhs_hbm.at[0, :, pl.ds(0, CHUNK)], rhs.at[0, :, pl.ds(0, CHUNK)], load_sem.at[1]),
     ]
+    others = pl.ds(CHUNK, width - CHUNK)
+    second = pltpu.make_async_copy(rhs_hbm.at[0, :, others], rhs.at[0, :, others], load_sem.at[10])
     maps = [
         pltpu.make_async_copy(target_hbm, target_ref, load_sem.at[7]),
         pltpu.make_async_copy(source_hbm, source_ref, load_sem.at[8]),
@@ -60,29 +63,45 @@
             pltpu.make_async_copy(inv_hbm.at[pl.ds(1, depth - 1)], inv.at[pl.ds(1, depth - 1)], load_sem.at[5]),
             pltpu.make_async_copy(rhs_hbm.at[pl.ds(1, depth - 1)], rhs.at[pl.ds(1, depth - 1)], load_sem.at[6]),
         ]
-    for load in early:
+    for load in early + [second]:
         load.start()
 
     barrier = pltpu.get_barrier_semaphore()
-    apart = [(o, e) for o, _, e in passes if (e, o) in [(a, b) for a, _, b in passes]]
-    strangers = sum((c == o).astype(jnp.int32) for o, _ in apart) if apart else 0
+    targets = n_col - 1
+    for owner, relay, end in passes:
+        targets = targets - (c == owner).astype(jnp.int32)
     for d in range(1, n_col):
         peer = lax.rem(c + d, n_col)
-        met = True
-        for o, e in apart:
-            met = met & jnp.logical_not((c == o) & (peer == e))
-
-        @pl.when(met)
+        writes_here = True
+        for owner, relay, end in passes:
+            writes_here = writes_here & jnp.logical_not((peer == owner) & (c == end))
+
+        @pl.when(writes_here)
         def _():
             pl.semaphore_signal(barrier, inc=1, device_id=(g, q, peer), device_id_type=MESH)
 
-    for e in range(n_grp):
-        for d in range(n_row):
-            if e or d:
-                pl.semaphore_signal(
-                    barrier, inc=1,
-                    device_id=(lax.rem(g + e, n_grp), lax.rem(q + d, n_row), c), device_id_type=MESH,
-                )
+    leads = (g == n_grp - 1) & (q == n_row - 1)
+    followers = n_grp * n_row - 1
+
+    @pl.when(jnp.logical_not(leads))
+    def _():
+        pl.semaphore_signal(barrier, inc=1, device_id=(n_grp - 1, n_row - 1, c), device_id_type=MESH)
+
+    def gather_plane():
+        @pl.when(leads)
+        def _():
+            for e in range(n_grp):
+                for d in range(n_row):
+                    if e or d:
+                        pl.semaphore_signal(
+                            plane_sem, inc=1,
+                            device_id=(lax.rem(g + e, n_grp), lax.rem(q + d, n_row), c), device_id_type=MESH,
+                        )
+
+    def await_plane():
+        @pl.when(jnp.logical_not(leads))
+        def _():
+            pl.semaphore_wait(plane_sem, 1)
 
     def tables(k, carry):
         count = count_ref[0, 0, 0, k]
@@ -253,12 +272,13 @@
 
     for load in early:
         load.wait()
+    solve(0, 0, 0, True)
+    pl.semaphore_wait(barrier, targets + jnp.where(leads, followers, 0))
+
+    send_direct(0)
+    second.wait()
     for load in maps + loads:
         load.start()
-    solve(0, 0, 0, True)
-    pl.semaphore_wait(barrier, n_col - 1 + n_grp * n_row - 1 - strangers)
-
-    send_direct(0)
 
     def first_level(w, carry):
         solve(w, 0, w, True)
@@ -266,6 +286,7 @@
         return carry
 
     lax.fori_loop(1, chunks, first_level, 0)
+    gather_plane()
     for load in maps:
         load.wait()
     lax.fori_loop(0, depth, tables, 0)
@@ -298,46 +319,45 @@
         def _():
             finish(later - steps)
 
+        pl.when(later > steps)(lambda: deliver(later - steps - 1))
+        pl.when(i >= BEHIND)(lambda: drain(i - BEHIND))
         return carry
 
+    def deliver(w):
+        owner = lax.rem(w, n_grp)
+
+        @pl.when(owner != g)
+        def _():
+            anc_copy(w, g).wait_recv()
+
+        anc_out[:, cols(w)] = anc_box[w]
+
+        @pl.when(owner == g)
+        def _():
+            for e in range(1, n_grp):
+                anc_copy(w, lax.rem(g + e, n_grp)).wait_send()
+
+    def drain(i):
+        each_direct(i, lambda copy, wait_turn: copy.wait_send())
+        relays(i, lambda arrived, onward: onward.wait_send())
+        to_g = jnp.where(i < (depth - 1) * chunks, g, lax.rem(lax.rem(i, chunks), n_grp))
+        for d in range(1, n_row):
+            rs_copy(i, g, q, to_g, lax.rem(q + d, n_row)).wait_send()
+
+        @pl.when(to_g != g)
+        def _():
+            rs_copy(i, g, q, to_g, q).wait_send()
+
+    await_plane()
     relays(0, pass_on)
     release(0)
     lax.fori_loop(0, steps, middle, 0)
     for w in range(chunks - LAG, chunks):
         finish(jnp.int32(w))
-
-    def deliver(w, carry):
-        owner = lax.rem(w, n_grp)
-
-        @pl.when(owner != g)
-        def _():
-            anc_copy(w, g).wait_recv()
-
-        anc_out[:, cols(w)] = anc_box[w]
-
-        @pl.when(owner == g)
-        def _():
-            for e in range(1, n_grp):
-                anc_copy(w, lax.rem(g + e, n_grp)).wait_send()
-
-        return carry
-
-    lax.fori_loop(0, chunks, deliver, 0)
-
-    def drain(i, carry):
-        each_direct(i, lambda copy, wait_turn: copy.wait_send())
-        relays(i, lambda arrived, onward: onward.wait_send())
-        to_g = jnp.where(i < (depth - 1) * chunks, g, lax.rem(lax.rem(i, chunks), n_grp))
-        for d in range(1, n_row):
-            rs_copy(i, g, q, to_g, lax.rem(q + d, n_row)).wait_send()
-
-        @pl.when(to_g != g)
-        def _():
-            rs_copy(i, g, q, to_g, q).wait_send()
-
-        return carry
-
-    lax.fori_loop(0, steps, drain, 0)
+    for i in range(steps - BEHIND, steps):
+        drain(jnp.int32(i))
+    for w in range(chunks - LAG - 1, chunks):
+        deliver(jnp.int32(w))
 
 
 def hand_over(sub_ref, anc_ref, sub_out, anc_out, sem):
@@ -387,7 +407,7 @@
             pltpu.SMEM((depth * slots,), jnp.int32),
             pltpu.SMEM((depth * codes,), jnp.int32),
             pltpu.SMEM((depth * slots,), jnp.int32),
-            dma((10,)),
+            dma((11,)),
             dma((steps, n_col)),
             dma((steps, n_col)),
             dma((steps, max(len(hops(n_col)), 1))),
@@ -395,6 +415,7 @@
             dma((steps, n_grp * n_row)),
             dma((chunks, n_grp)),
             dma((chunks,)),
+            pltpu.SemaphoreType.REGULAR,
         ],
         compiler_params=pltpu.CompilerParams(
             collective_id=0, has_side_effects=True, vmem_limit_bytes=67_043_328 - 4 * (depth + 1) * size * width

time: 70.1 us -> 68.6 us (0.979)
  Pallas kernels: 69.3 us -> 67.8 us
    pallas_call x1, Pallas kernels: 68 us -> 66.5 us  [on_device(): pl.pallas_call(functools.partial(kernel, n_grp, n_row, n_col), out_shape=...]
where the time goes in v3:
time: 68.6 us; the launch traced here: 68.5 us
  Pallas kernels  67.8 us (99%)
    pallas_call x1, Pallas kernels, on_device(): pl.pallas_call(functools.partial(kernel, n_grp, n_row, n_col), out_shape=...  66.5 us

profile of v3, /device:TPU:0, one launch (start us, length us, event | category | flops | bytes accessed | tf_op | source)
XLA Modules:
  0.0 68.5 jit_solution(3182136394104528425)
XLA Ops:
  0.6 66.5 %shard_map.95 = (f32[3,256,512]{2,1,0:T(8,128)S(1)}, f32[256,512]{1,0:T(8,128)S(1)}) custom-call(s32[3,1,16]{2,1,0:T(1,128)} %bitcast.16, s32[3,1,16]{2,1,0:T(1,128)} %bitcast.17, s32[1,1,1,3]{3,2,1,0:T(1,128)} %count_hbm.1, f32[3,256,512]{2,1,0:T(8,128)} %bitcast.12, f32[3,256,256]{2,1,0:T(8,128)} %bitcast.13, f32[256,512]{1,0:T(8,128)} %bitcast.14, ...), custom_call_target="tpu_custom_call" | custom-call | tf_op jit(solution)/shard_map/pallas_call | solution.py:383
  67.1 1.3 %shard_map.96 = (f32[3,256,512]{2,1,0:T(8,128)}, f32[256,512]{1,0:T(8,128)}) custom-call(f32[3,256,512]{2,1,0:T(8,128)S(1)} %get-tuple-element.6.sub_ref, f32[256,512]{1,0:T(8,128)S(1)} %get-tuple-element.7.anc_ref), custom_call_target="tpu_custom_call" | custom-call | tf_op jit(solution)/shard_map/pallas_call | solution.py:429

commit v4 on v3

--- a/solution.py
+++ b/solution.py
@@ -315,11 +315,11 @@
             solve(later, later // chunks, lax.rem(later, chunks), False)
             send_direct(later)
 
-        @pl.when(later >= steps)
-        def _():
-            finish(later - steps)
-
-        pl.when(later > steps)(lambda: deliver(later - steps - 1))
+        @pl.when(later >= steps + 1)
+        def _():
+            finish(later - steps - 1)
+
+        pl.when(later >= steps + 3)(lambda: deliver(later - steps - 3))
         pl.when(i >= BEHIND)(lambda: drain(i - BEHIND))
         return carry
 
@@ -352,11 +352,11 @@
     relays(0, pass_on)
     release(0)
     lax.fori_loop(0, steps, middle, 0)
-    for w in range(chunks - LAG, chunks):
+    for w in range(max(chunks - LAG - 1, 0), chunks):
         finish(jnp.int32(w))
     for i in range(steps - BEHIND, steps):
         drain(jnp.int32(i))
-    for w in range(chunks - LAG - 1, chunks):
+    for w in range(max(chunks - LAG - 3, 0), chunks):
         deliver(jnp.int32(w))
 
 

time: 68.6 us -> 67.2 us (0.980)
  Pallas kernels: 67.8 us -> 66.4 us
    pallas_call x1, Pallas kernels: 66.5 us -> 65.1 us  [on_device(): pl.pallas_call(functools.partial(kernel, n_grp, n_row, n_col), out_shape=...]
where the time goes in v4:
time: 67.2 us; the launch traced here: 67 us
  Pallas kernels  66.4 us (99%)
    pallas_call x1, Pallas kernels, on_device(): pl.pallas_call(functools.partial(kernel, n_grp, n_row, n_col), out_shape=...  65.1 us

profile of v4, /device:TPU:0, one launch (start us, length us, event | category | flops | bytes accessed | tf_op | source)
XLA Modules:
  0.0 67.0 jit_solution(12201144793888099471)
XLA Ops:
  0.6 65.1 %shard_map.95 = (f32[3,256,512]{2,1,0:T(8,128)S(1)}, f32[256,512]{1,0:T(8,128)S(1)}) custom-call(s32[3,1,16]{2,1,0:T(1,128)} %bitcast.16, s32[3,1,16]{2,1,0:T(1,128)} %bitcast.17, s32[1,1,1,3]{3,2,1,0:T(1,128)} %count_hbm.1, f32[3,256,512]{2,1,0:T(8,128)} %bitcast.12, f32[3,256,256]{2,1,0:T(8,128)} %bitcast.13, f32[256,512]{1,0:T(8,128)} %bitcast.14, ...), custom_call_target="tpu_custom_call" | custom-call | tf_op jit(solution)/shard_map/pallas_call | solution.py:383
  65.7 1.3 %shard_map.96 = (f32[3,256,512]{2,1,0:T(8,128)}, f32[256,512]{1,0:T(8,128)}) custom-call(f32[3,256,512]{2,1,0:T(8,128)S(1)} %get-tuple-element.6.sub_ref, f32[256,512]{1,0:T(8,128)S(1)} %get-tuple-element.7.anc_ref), custom_call_target="tpu_custom_call" | custom-call | tf_op jit(solution)/shard_map/pallas_call | solution.py:429

commit v5 on v4

--- a/solution.py
+++ b/solution.py
@@ -27,7 +27,7 @@
     target_hbm, source_hbm, count_hbm,
     rhs_hbm, inv_hbm, anc_rhs_hbm, anc_inv_hbm, tiles_hbm,
     sub_out, anc_out,
-    rhs, inv, anc_rhs, anc_inv, tiles,
+    rhs, inv, anc_rhs, anc_inv, tiles, wide,
     gathered, fetched, chain, pending, outbox, inbox, anc_box,
     target_ref, source_ref, count_ref, prev_s, last_s, src_s,
     load_sem, ag_send, ag_recv, fwd_send, rs_send, rs_recv, anc_send, anc_recv, plane_sem,
@@ -80,12 +80,12 @@
         def _():
             pl.semaphore_signal(barrier, inc=1, device_id=(g, q, peer), device_id_type=MESH)
 
-    leads = (g == n_grp - 1) & (q == n_row - 1)
+    leads = (g == 0) & (q == n_row - 1)
     followers = n_grp * n_row - 1
 
     @pl.when(jnp.logical_not(leads))
     def _():
-        pl.semaphore_signal(barrier, inc=1, device_id=(n_grp - 1, n_row - 1, c), device_id_type=MESH)
+        pl.semaphore_signal(barrier, inc=1, device_id=(0, n_row - 1, c), device_id_type=MESH)
 
     def gather_plane():
         @pl.when(leads)
@@ -190,7 +190,14 @@
         )
 
     def full_dot(a, b):
-        return jnp.dot(a, b, precision=lax.Precision.HIGHEST, preferred_element_type=jnp.float32)
+        high = b.astype(jnp.bfloat16)
+        low = (b - high.astype(jnp.float32)).astype(jnp.bfloat16)
+        return jnp.dot(a, jnp.concatenate([high, low, high], axis=0), preferred_element_type=jnp.float32)
+
+    def widen(a):
+        high = a.astype(jnp.bfloat16)
+        low = (a - high.astype(jnp.float32)).astype(jnp.bfloat16)
+        return jnp.concatenate([high, high, low], axis=1)
 
     def solve(i, k, w, first):
         rest = rhs[k, :, cols(w)]
@@ -202,7 +209,7 @@
                 rs_copy(back, g, other, g, q).wait_recv()
                 total = total + inbox[back, g * n_row + other].astype(jnp.float32)
             rest = rest - total
-        answer = full_dot(inv[k], rest)
+        answer = full_dot(wide[k], rest)
         sub_out[k, :, cols(w)] = answer
         gathered[i, c] = answer.astype(jnp.bfloat16)
 
@@ -211,8 +218,9 @@
         onward.start()
 
     def spread(i, k, w):
+        fetched[c] = gathered[i, c]
         for d in range(1, n_col):
-            other = lax.rem(c + d, n_col)
+            other = lax.rem(c + jnp.where(c < n_col // 2, d, n_col - d), n_col)
             passed = False
             for owner, relay, end in passes:
                 passed = passed | ((c == relay) & (other == owner))
@@ -221,8 +229,7 @@
             def _():
                 ag_copy(i, other, c).wait_recv()
 
-        for s in range(n_col):
-            fetched[s] = gathered[i, s]
+            fetched[other] = gathered[i, other]
 
         for j in range(slots):
             product = jnp.dot(
@@ -266,12 +273,13 @@
                         other_g, other_q = lax.rem(g + e, n_grp), lax.rem(q + d, n_row)
                         rs_copy(i, other_g, other_q, g, q).wait_recv()
                         total = total + inbox[i, other_g * n_row + other_q].astype(jnp.float32)
-            anc_box[w] = full_dot(anc_inv[...], anc_rhs[:, cols(w)] - total)
+            anc_box[w] = full_dot(wide[depth], anc_rhs[:, cols(w)] - total)
             for e in range(1, n_grp):
                 anc_copy(w, lax.rem(g + e, n_grp)).start()
 
     for load in early:
         load.wait()
+    wide[0] = widen(inv[0])
     solve(0, 0, 0, True)
     pl.semaphore_wait(barrier, targets + jnp.where(leads, followers, 0))
 
@@ -299,6 +307,9 @@
     lax.fori_loop(0, chunks * codes, clear, 0)
     for load in loads:
         load.wait()
+    for k in range(1, depth):
+        wide[k] = widen(inv[k])
+    wide[depth] = widen(anc_inv[...])
 
     def middle(i, carry):
         spread(i, i // chunks, lax.rem(i, chunks))
@@ -394,6 +405,7 @@
             pltpu.VMEM((size, width), f32),
             pltpu.VMEM((size, size), f32),
             pltpu.VMEM((depth, slots, size, size), bf16),
+            pltpu.VMEM((depth + 1, size, 3 * size), bf16),
             pltpu.VMEM((steps, n_col, size, CHUNK), bf16),
             pltpu.VMEM((n_col, size, CHUNK), bf16),
             pltpu.VMEM((slots + 1, size, CHUNK), f32),

time: 67.2 us -> 66.9 us (level)
  no operation moved by 1% of the time
where the time goes in v5:
time: 66.9 us; the launch traced here: 66.8 us
  Pallas kernels  66.2 us (99%)
    pallas_call x1, Pallas kernels, on_device(): pl.pallas_call(functools.partial(kernel, n_grp, n_row, n_col), out_shape=...  64.8 us

profile of v5, /device:TPU:0, one launch (start us, length us, event | category | flops | bytes accessed | tf_op | source)
XLA Modules:
  0.0 66.8 jit_solution(6005107409826970550)
XLA Ops:
  0.6 64.8 %shard_map.95 = (f32[3,256,512]{2,1,0:T(8,128)S(1)}, f32[256,512]{1,0:T(8,128)S(1)}) custom-call(s32[3,1,16]{2,1,0:T(1,128)} %bitcast.16, s32[3,1,16]{2,1,0:T(1,128)} %bitcast.17, s32[1,1,1,3]{3,2,1,0:T(1,128)} %count_hbm.1, f32[3,256,512]{2,1,0:T(8,128)} %bitcast.12, f32[3,256,256]{2,1,0:T(8,128)} %bitcast.13, f32[256,512]{1,0:T(8,128)} %bitcast.14, ...), custom_call_target="tpu_custom_call" | custom-call | tf_op jit(solution)/shard_map/pallas_call | solution.py:394
  65.5 1.3 %shard_map.96 = (f32[3,256,512]{2,1,0:T(8,128)}, f32[256,512]{1,0:T(8,128)}) custom-call(f32[3,256,512]{2,1,0:T(8,128)S(1)} %get-tuple-element.6.sub_ref, f32[256,512]{1,0:T(8,128)S(1)} %get-tuple-element.7.anc_ref), custom_call_target="tpu_custom_call" | custom-call | tf_op jit(solution)/shard_map/pallas_call | solution.py:441

commit v6 on v5

--- a/solution.py
+++ b/solution.py
@@ -326,11 +326,6 @@
             solve(later, later // chunks, lax.rem(later, chunks), False)
             send_direct(later)
 
-        @pl.when(later >= steps + 1)
-        def _():
-            finish(later - steps - 1)
-
-        pl.when(later >= steps + 3)(lambda: deliver(later - steps - 3))
         pl.when(i >= BEHIND)(lambda: drain(i - BEHIND))
         return carry
 
@@ -363,11 +358,11 @@
     relays(0, pass_on)
     release(0)
     lax.fori_loop(0, steps, middle, 0)
-    for w in range(max(chunks - LAG - 1, 0), chunks):
+    for w in range(chunks):
         finish(jnp.int32(w))
     for i in range(steps - BEHIND, steps):
         drain(jnp.int32(i))
-    for w in range(max(chunks - LAG - 3, 0), chunks):
+    for w in range(chunks):
         deliver(jnp.int32(w))
 
 

time: 66.9 us -> 66.9 us (level)
  no operation moved by 1% of the time
where the time goes in v6:
time: 66.9 us; the launch traced here: 66.8 us
  Pallas kernels  66.2 us (99%)
    pallas_call x1, Pallas kernels, on_device(): pl.pallas_call(functools.partial(kernel, n_grp, n_row, n_col), out_shape=...  64.8 us

profile of v6, /device:TPU:0, one launch (start us, length us, event | category | flops | bytes accessed | tf_op | source)
XLA Modules:
  0.0 66.8 jit_solution(2075830754624513420)
XLA Ops:
  0.6 64.8 %shard_map.95 = (f32[3,256,512]{2,1,0:T(8,128)S(1)}, f32[256,512]{1,0:T(8,128)S(1)}) custom-call(s32[3,1,16]{2,1,0:T(1,128)} %bitcast.16, s32[3,1,16]{2,1,0:T(1,128)} %bitcast.17, s32[1,1,1,3]{3,2,1,0:T(1,128)} %count_hbm.1, f32[3,256,512]{2,1,0:T(8,128)} %bitcast.12, f32[3,256,256]{2,1,0:T(8,128)} %bitcast.13, f32[256,512]{1,0:T(8,128)} %bitcast.14, ...), custom_call_target="tpu_custom_call" | custom-call | tf_op jit(solution)/shard_map/pallas_call | solution.py:389
  65.5 1.3 %shard_map.96 = (f32[3,256,512]{2,1,0:T(8,128)}, f32[256,512]{1,0:T(8,128)}) custom-call(f32[3,256,512]{2,1,0:T(8,128)S(1)} %get-tuple-element.6.sub_ref, f32[256,512]{1,0:T(8,128)S(1)} %get-tuple-element.7.anc_ref), custom_call_target="tpu_custom_call" | custom-call | tf_op jit(solution)/shard_map/pallas_call | solution.py:436
